TPU v7x, 32 devices: a whole 2x2x4 slice. The times are simulated.
32 devices in a mesh: section: 2 (over x), tensor: 2 (over y), expert: 8 (over z, core).
Axes of the slice: x: 2, y: 2, z: 4, core: 2. Of those that a mesh axis runs over, the one named last changes fastest.
Arguments:
- saved_inputs: bfloat16 [2, 2, 512, 2048], P('section', None, 'expert', 'tensor'), may hold values from -64 to 64
- cot_in: bfloat16 [2, 512, 2048], P('section', 'expert', 'tensor'), may hold values from -6 to 6
- loss_grad: bfloat16 [512, 2048], P('expert', 'tensor'), may hold values from -6 to 6
- expert_ids: int32 [2, 2, 512, 2], P('section', None, 'expert'), may hold values from 0 to 3, all different within a row; in each aligned block of 64 rows (0 to 63, 64 to 127, ..., all dimensions but the last counted through in order) at most 48 rows name the same one
- route_weights: float32 [2, 2, 512, 2], P('section', None, 'expert'), may hold values from 0.05 to 0.5
- norm_gain: float32 [2, 2048], P('section', 'tensor'), may hold values from 0.12 to 8
- w_gate: bfloat16 [2, 8, 2048, 384], P('section', 'expert', 'tensor'), may hold values from -0.125 to 0.125
- w_up: bfloat16 [2, 8, 2048, 384], P('section', 'expert', 'tensor'), may hold values from -0.125 to 0.125
- w_down: bfloat16 [2, 8, 384, 2048], P('section', 'expert', None, 'tensor'), may hold values from -0.21875 to 0.21875
Outputs:
- input_grads: bfloat16 [2, 2, 512, 2048], P('section', None, 'expert', 'tensor')
Inputs may be any that keep to these rules, and one draw needn't show every extreme that they name: `expert_ids`: each row names 2 different experts. Within each aligned block of 64 rows (the rows of one device in one micro-batch of one layer) no expert is named by more than 48 rows, and in some blocks one expert is named by exactly 48.
All inputs are finite; a program needn't handle non-finite values.
Results may differ from a plain program's by a relative error of at most 0.028.
Values may be sent and summed in bfloat16 or wider, within the bound.
A program may use at most 64 MiB of HBM per device.

v0:
```python
import jax
import jax.numpy as jnp
from jax import lax
from jax.experimental import pallas as pl
from jax.experimental.pallas import tpu as pltpu
from jax.sharding import PartitionSpec as P

epsilon = 1e-06
MESH = pl.DeviceIdType.MESH
bf16 = jnp.bfloat16
f32 = jnp.float32


def contract_last(left, right):
    return lax.dot_general(left, right, (((1,), (1,)), ((), ())), preferred_element_type=f32)


def contract_first(left, right):
    return lax.dot_general(left, right, (((0,), (0,)), ((), ())), preferred_element_type=f32)


def dot(left, right):
    return jnp.dot(left, right, preferred_element_type=f32)


def make_kernel(sections, tensors, experts, capacity):

    def kernel(
        saved, cot_in, loss_grad, ids, weights, gain, wg_hbm, wu_hbm, wd_hbm, out,
        wg, wu, wd, w_sem, choose, picked, rows_out, rows, part_gu, part_h,
        y_send_gu, y_recv_gu, y_send_h, y_recv_h, grads, piece, pair_send, pair_recv,
        ret_send, ret_recv, sq_send, sq_recv, in_send, in_recv, sec_recv,
        d_s, d_r, f_s, f_r, y_s, y_r, a_s, a_r, p_s, p_r, r_s, r_r, q_s, q_r, i_s, i_r, c_s, c_r,
    ):
        s = lax.axis_index("section")
        t = lax.axis_index("tensor")
        x = lax.axis_index("expert")
        e, q = x // 2, x % 2
        ot, oq = 1 - t, 1 - q
        tok = saved.shape[2]
        feat = saved.shape[3]
        top = ids.shape[2]
        hid = wg.shape[1]
        model = feat * tensors

        loads = [
            pltpu.make_async_copy(wd_hbm.at[0, 0], wd, w_sem.at[0]),
            pltpu.make_async_copy(wg_hbm.at[0, 0], wg, w_sem.at[1]),
            pltpu.make_async_copy(wu_hbm.at[0, 0], wu, w_sem.at[2]),
        ]
        for load in loads:
            load.start()

        def expert_at(j):
            return lax.rem(e + j, experts)

        def source_at(j):
            return lax.rem(e + experts - j, experts)

        lane_peer = lambda chip: (s, t, 2 * chip + q)
        partner = (s, t, 2 * e + oq)
        y_peer = (s, ot, x)

        barrier = pltpu.get_barrier_semaphore()
        greet = [lane_peer(expert_at(j)) for j in range(1, experts)] + [partner, y_peer]
        for device in greet:
            pl.semaphore_signal(barrier, inc=1, device_id=device, device_id_type=MESH)

        @pl.when(s > 0)
        def _():
            pl.semaphore_signal(barrier, inc=1, device_id=(s - 1, t, x), device_id_type=MESH)

        @pl.when(s < sections - 1)
        def _():
            pl.semaphore_signal(barrier, inc=1, device_id=(s + 1, t, x), device_id_type=MESH)

        def remote(src, dst, send, recv, device):
            return pltpu.make_async_remote_copy(
                src_ref=src, dst_ref=dst, send_sem=send, recv_sem=recv,
                device_id=device, device_id_type=MESH,
            )

        def direct(m, k, j):
            return remote(
                rows_out.at[m, k, j], rows.at[m, k, j, q], d_s.at[m, k, j], d_r.at[m, k, j],
                lane_peer(expert_at(j)),
            )

        def forward(m, k, j):
            return remote(
                rows.at[m, k, j, q], rows.at[m, k, j, q], f_s.at[m, k, j], f_r.at[m, k, j], partner
            )

        def exchange(m, k, j):
            src, dst = ((y_send_gu, y_recv_gu), (y_send_h, y_recv_h))[k]
            return remote(src.at[m, j], dst.at[m, j], y_s.at[m, k, j], y_r.at[m, k, j], y_peer)

        def share(m, j):
            return remote(
                grads.at[m, j, t], grads.at[m, j, t], a_s.at[m, j], a_r.at[m, j], y_peer
            )

        def pair(m, j):
            return remote(
                pair_send.at[m, j], pair_recv.at[m, j], p_s.at[m, j], p_r.at[m, j], partner
            )

        def give_back(m, j):
            return remote(
                ret_send.at[m, j], ret_recv.at[m, j], r_s.at[m, j], r_r.at[m, j],
                lane_peer(source_at(j)),
            )

        def squares_copy():
            return remote(sq_send, sq_recv, q_s, q_r, y_peer)

        def inner_copy(m):
            return remote(in_send.at[m], in_recv.at[m], i_s.at[m], i_r.at[m], y_peer)

        def section_copy():
            return remote(out.at[0, 0], sec_recv, c_s, c_r, (s - 1, t, x))

        started = []

        def start(copy):
            copy.start()
            started.append(copy)

        height = max(8, experts)
        lane = lax.broadcasted_iota(jnp.int32, (tok, 128), 1)
        named = e + lax.broadcasted_iota(jnp.int32, (height, tok), 0)
        named = jnp.where(named >= experts, named - experts, named)
        later = (
            lax.broadcasted_iota(jnp.int32, (tok, tok), 0)
            < lax.broadcasted_iota(jnp.int32, (tok, tok), 1)
        ).astype(f32).astype(bf16)
        slot = lax.broadcasted_iota(jnp.int32, (capacity, tok), 0).astype(f32)
        for m in range(2):
            hit = jnp.zeros((height, tok), f32)
            weight = jnp.zeros((height, tok), f32)
            for k in range(top):
                same = (ids[0, m, k : k + 1, :] == named).astype(f32)
                hit = hit + same
                weight = weight + same * weights[0, m, k : k + 1, :]
            position = dot(hit.astype(bf16), later)
            for j in range(experts):
                chosen = (position[j : j + 1] == slot).astype(f32) * hit[j : j + 1]
                choose[m, j] = chosen.astype(bf16)
                picked[m, j] = jnp.broadcast_to(
                    jnp.sum(chosen * weight[j : j + 1], axis=1, keepdims=True), (capacity, 128)
                )
        square = []
        for m in range(2):
            values = saved[0, m].astype(f32)
            square.append(jnp.sum(values * values, axis=1, keepdims=True))
        sq_send[...] = jnp.where(lane < 64, square[0], square[1])

        neighbours = (s > 0).astype(jnp.int32) + (s < sections - 1).astype(jnp.int32)
        pl.semaphore_wait(barrier, len(greet) + neighbours)

        start(squares_copy())

        def dispatch(m, k, j, value):
            packed = dot(choose[m, j], value)
            if k == 1:
                packed = picked[m, j][:, :1] * packed
            if j == 0:
                rows[m, k, j, q] = packed.astype(bf16)
                start(forward(m, k, j))
            else:
                rows_out[m, k, j] = packed.astype(bf16)
                start(direct(m, k, j))

        js = list(range(experts))
        near = js[1 : experts // 2 + 1] + [0]
        far = js[experts // 2 + 1 :]
        for j in near:
            dispatch(0, 1, j, cot_in[0])
        squares_copy().wait_recv()
        total = sq_send[...] + sq_recv[...]
        roots = [
            jnp.sqrt(total[:, 64 * m : 64 * m + 1] / model + epsilon) for m in range(2)
        ]

        def normed_of(m):
            return saved[0, m].astype(f32) / roots[m]

        def expert_input(m):
            return (normed_of(m) * gain[...]).astype(bf16)

        value = expert_input(0)
        for j in near:
            dispatch(0, 0, j, value)
        for j in far:
            dispatch(0, 1, j, cot_in[0])
            dispatch(0, 0, j, value)

        for load in loads:
            load.wait()

        def receive(m, k, j):
            if j > 0:
                direct(m, k, j).wait_recv()
                start(forward(m, k, j))

        def consume(m, k, j):
            forward(m, k, j).wait_recv()
            flat = rows[m, k, j].reshape(2 * capacity, feat)
            if k == 0:
                part_gu[m, j, :, :, :hid] = dot(flat, wg[...]).reshape(2, capacity, hid)
                part_gu[m, j, :, :, hid:] = dot(flat, wu[...]).reshape(2, capacity, hid)
                y_send_gu[m, j] = part_gu[m, j, ot].astype(bf16)
            else:
                part_h[m, j] = contract_last(flat, wd[...]).reshape(2, capacity, hid)
                y_send_h[m, j] = part_h[m, j, ot].astype(bf16)
            start(exchange(m, k, j))

        def stream(items):
            last = None
            for item in items:
                receive(*item)
                if last is not None:
                    consume(*last)
                last = item
            consume(*last)

        def activate(m, j):
            exchange(m, 0, j).wait_recv()
            exchange(m, 1, j).wait_recv()
            both = part_gu[m, j, t] + y_recv_gu[m, j].astype(f32)
            hidden = part_h[m, j, t] + y_recv_h[m, j].astype(f32)
            gate, up = both[:, :hid], both[:, hid:]
            sigma = jax.nn.sigmoid(gate)
            grads[m, j, t, :, :hid] = (
                hidden * up * (sigma * (1.0 + gate * (1.0 - sigma)))
            ).astype(bf16)
            grads[m, j, t, :, hid:] = (hidden * (gate * sigma)).astype(bf16)
            start(share(m, j))

        def pieces(m, j):
            share(m, j).wait_recv()
            flat = grads[m, j].reshape(2 * capacity, 2 * hid)
            done = contract_last(flat[:, :hid], wg[...]) + contract_last(flat[:, hid:], wu[...])
            piece[m, j] = done.reshape(2, capacity, feat)
            pair_send[m, j] = piece[m, j, oq].astype(bf16)
            start(pair(m, j))

        def finish(m, j):
            pair(m, j).wait_recv()
            summed = (piece[m, j, q] + pair_recv[m, j].astype(f32)).astype(bf16)
            if j == 0:
                ret_recv[m, j] = summed
            else:
                ret_send[m, j] = summed
                start(give_back(m, j))

        def pipeline(m, kinds, between=()):
            stream([(m, k, j) for k in kinds for j in js])
            for j in js[1:] + [0]:
                activate(m, j)
            if between:
                stream(between)
            last = None
            for j in js[1:] + [0]:
                pieces(m, j)
                if last is not None:
                    finish(m, last)
                last = j
            finish(m, last)

        def combine(m, incoming):
            cot = contract_first(choose[m, 0], ret_recv[m, 0])
            for j in range(1, experts):
                give_back(m, j).wait_recv()
                cot = cot + contract_first(choose[m, j], ret_recv[m, j])
            scaled = gain[...] * cot
            normed = normed_of(m)
            own = jnp.sum(normed * scaled, axis=1, keepdims=True)
            in_send[m] = jnp.broadcast_to(own, (tok, 128))
            start(inner_copy(m))
            inner_copy(m).wait_recv()
            inner = (in_send[m] + in_recv[m])[:, :1]
            out[0, m] = (
                incoming + (scaled - normed * (inner / model)) / roots[m]
            ).astype(bf16)

        pipeline(0, (1, 0))
        value = expert_input(1)
        for j in js[1:] + [0]:
            dispatch(1, 0, j, value)
        combine(0, cot_in[0].astype(f32))

        @pl.when(s > 0)
        def _():
            section_copy().start()

        stream([(1, 0, j) for j in js[: experts // 2]])

        @pl.when(s < sections - 1)
        def _():
            section_copy().wait_recv()

        @pl.when(s == sections - 1)
        def _():
            sec_recv[...] = loss_grad[...]

        for j in js[1:] + [0]:
            dispatch(1, 1, j, sec_recv[...])
        stream([(1, 0, j) for j in js[experts // 2 :]])
        pipeline(1, (1,))
        combine(1, sec_recv[...].astype(f32))

        for copy in started:
            copy.wait_send()

        @pl.when(s > 0)
        def _():
            section_copy().wait_send()

    return kernel


def solution(mesh):
    sections, tensors = mesh.shape["section"], mesh.shape["tensor"]
    experts = mesh.shape["expert"] // 2

    def local(saved, cot_in, loss_grad, ids, weights, gain, wg, wu, wd):
        tok, feat = saved.shape[2], saved.shape[3]
        hid = wg.shape[3]
        named = 3 * tok * ids.shape[3] // (2 * experts)
        cap = -(-named // 16) * 16
        vmem = pl.BlockSpec(memory_space=pltpu.VMEM)
        hbm = pl.BlockSpec(memory_space=pl.ANY)
        dma = pltpu.SemaphoreType.DMA
        scratch = [
            pltpu.VMEM((feat, hid), bf16), pltpu.VMEM((feat, hid), bf16),
            pltpu.VMEM((hid, feat), bf16), dma((3,)),
            pltpu.VMEM((2, experts, cap, tok), bf16), pltpu.VMEM((2, experts, cap, 128), f32),
            pltpu.VMEM((2, 2, experts, cap, feat), bf16),
            pltpu.VMEM((2, 2, experts, 2, cap, feat), bf16),
            pltpu.VMEM((2, experts, 2, cap, 2 * hid), f32),
            pltpu.VMEM((2, experts, 2, cap, hid), f32),
            pltpu.VMEM((2, experts, cap, 2 * hid), bf16),
            pltpu.VMEM((2, experts, cap, 2 * hid), bf16),
            pltpu.VMEM((2, experts, cap, hid), bf16),
            pltpu.VMEM((2, experts, cap, hid), bf16),
            pltpu.VMEM((2, experts, 2, cap, 2 * hid), bf16),
            pltpu.VMEM((2, experts, 2, cap, feat), f32),
            pltpu.VMEM((2, experts, cap, feat), bf16),
            pltpu.VMEM((2, experts, cap, feat), bf16),
            pltpu.VMEM((2, experts, cap, feat), bf16),
            pltpu.VMEM((2, experts, cap, feat), bf16),
            pltpu.VMEM((tok, 128), f32), pltpu.VMEM((tok, 128), f32),
            pltpu.VMEM((2, tok, 128), f32), pltpu.VMEM((2, tok, 128), f32),
            pltpu.VMEM((tok, feat), bf16),
        ]
        for shape in [(2, 2, experts)] * 6 + [(2, experts)] * 6:
            scratch.append(dma(shape))
        scratch += [dma, dma, dma((2,)), dma((2,)), dma, dma]
        return pl.pallas_call(
            make_kernel(sections, tensors, experts, cap),
            out_shape=jax.ShapeDtypeStruct((1, 2, tok, feat), bf16),
            in_specs=[vmem] * 6 + [hbm] * 3,
            out_specs=vmem,
            scratch_shapes=scratch,
            compiler_params=pltpu.CompilerParams(
                collective_id=0, has_side_effects=True, vmem_limit_bytes=62 * 1024 * 1024
            ),
            name="expert_back",
        )(
            saved, cot_in, loss_grad, ids.transpose(0, 1, 3, 2), weights.transpose(0, 1, 3, 2),
            gain, wg, wu, wd,
        )

    in_specs = (
        P("section", None, "expert", "tensor"),
        P("section", "expert", "tensor"),
        P("expert", "tensor"),
        P("section", None, "expert", None),
        P("section", None, "expert", None),
        P("section", "tensor"),
        P("section", "expert", "tensor", None),
        P("section", "expert", "tensor", None),
        P("section", "expert", None, "tensor"),
    )
    out_specs = P("section", None, "expert", "tensor")
    return jax.shard_map(local, mesh=mesh, in_specs=in_specs, out_specs=out_specs, check_vma=False)
```

profile of v0, /device:TPU:0, one launch (start us, length us, event | category | flops | bytes accessed | tf_op | source)
XLA Modules:
  0.0 90.9 jit_solution(4948665008938409633)
XLA Ops:
  0.0 89.2 %expert_back.1 = bf16[1,2,64,1024]{3,2,1,0:T(8,128)(2,1)} custom-call(bf16[1,2,64,1024]{3,2,1,0:T(8,128)(2,1)} %saved.1, bf16[1,64,1024]{2,1,0:T(8,128)(2,1)} %cot_in.1, bf16[64,1024]{1,0:T(8,128)(2,1)} %loss_grad.1, s32[1,2,2,64]{3,2,1,0:T(2,128)} %bitcast.2, f32[1,2,2,64]{3,2,1,0:T(2,128)} %bitcast.3, f32[1,1024]{1,0:T(1,128)} %gain.1, ...), custom_call_target="tpu_custom_call" | custom-call | tf_op jit(solution)/shard_map/expert_back/pallas_call | solution.py:360
  89.2 1.7 %copy.11 = bf16[1,2,64,1024]{3,2,1,0:T(8,128)(2,1)} copy(bf16[1,2,64,1024]{3,2,1,0:T(8,128)(2,1)} %expert_back.1) | data formatting | bytes 524288
where the time goes:
time: 91 us; the launch traced here: 90.9 us
  Pallas kernels  89.2 us (98%)
  local copies, waits for them, and re-layouts  1.67 us (2%)
    pallas_call x1, Pallas kernels, local(): pl.pallas_call(make_kernel(sections, tensors, experts, cap), out_shape=ja...  89.2 us

commit v1 on v0

v1 whole, which is shorter than its diff:
```python
import jax
import jax.numpy as jnp
from jax import lax
from jax.experimental import pallas as pl
from jax.experimental.pallas import tpu as pltpu
from jax.sharding import PartitionSpec as P

epsilon = 1e-06
MESH = pl.DeviceIdType.MESH
bf16 = jnp.bfloat16
f32 = jnp.float32


def contract_last(left, right):
    return lax.dot_general(left, right, (((1,), (1,)), ((), ())), preferred_element_type=f32)


def contract_first(left, right):
    return lax.dot_general(left, right, (((0,), (0,)), ((), ())), preferred_element_type=f32)


def dot(left, right):
    return jnp.dot(left, right, preferred_element_type=f32)


def make_kernel(sections, tensors, experts, capacity):

    def kernel(
        saved, cot_in, loss_grad, ids, weights, gain, wg_hbm, wu_hbm, wd_hbm, out,
        wgu, wd, w_sem, choose, picked, rows_out, rows, part_gu, part_h,
        gu_send, gu_recv, h_send, h_recv, grads, ret_send, ret_recv,
        sc_send, sc_recv, sq_send, sq_recv, sec_recv,
        w_s, w_r, d_s, d_r, y_s, y_r, r_s, r_r, v_s, v_r, q_s, q_r, c_s, c_r,
    ):
        s = lax.axis_index("section")
        t = lax.axis_index("tensor")
        x = lax.axis_index("expert")
        e, q = x // 2, x % 2
        tok = saved.shape[2]
        feat = saved.shape[3]
        top = ids.shape[2]
        hid = wd_hbm.shape[2]
        model = feat * tensors
        js = list(range(experts))

        loads = [
            pltpu.make_async_copy(wd_hbm.at[0, 0], wd.at[0:hid], w_sem.at[0]),
            pltpu.make_async_copy(wg_hbm.at[0, 0], wgu.at[:, 0:hid], w_sem.at[1]),
            pltpu.make_async_copy(wu_hbm.at[0, 0], wgu.at[:, 2 * hid : 3 * hid], w_sem.at[2]),
        ]
        for load in loads:
            load.start()

        def expert_at(j):
            other, bit = e, 1
            while bit < experts:
                if j & bit:
                    other = other + bit - 2 * bit * ((e // bit) % 2)
                bit *= 2
            return other

        lane_peer = lambda j: (s, t, 2 * expert_at(j) + q)
        partner = (s, t, 2 * e + 1 - q)
        y_peer = (s, 1 - t, x)

        barrier = pltpu.get_barrier_semaphore()
        greet = [lane_peer(j) for j in js[1:]] + [partner, y_peer]
        for device in greet:
            pl.semaphore_signal(barrier, inc=1, device_id=device, device_id_type=MESH)

        @pl.when(s > 0)
        def _():
            pl.semaphore_signal(barrier, inc=1, device_id=(s - 1, t, x), device_id_type=MESH)

        @pl.when(s < sections - 1)
        def _():
            pl.semaphore_signal(barrier, inc=1, device_id=(s + 1, t, x), device_id_type=MESH)

        def remote(src, dst, send, recv, device):
            return pltpu.make_async_remote_copy(
                src_ref=src, dst_ref=dst, send_sem=send, recv_sem=recv,
                device_id=device, device_id_type=MESH,
            )

        def weight_copy(i):
            ref = (
                (wd.at[0:hid], wd.at[hid : 2 * hid]),
                (wgu.at[:, 0:hid], wgu.at[:, hid : 2 * hid]),
                (wgu.at[:, 2 * hid : 3 * hid], wgu.at[:, 3 * hid : 4 * hid]),
            )[i]
            return remote(ref[0], ref[1], w_s.at[i], w_r.at[i], partner)

        def direct(m, k, j):
            return remote(
                rows_out.at[m, k, j], rows.at[m, k, j], d_s.at[m, k, j], d_r.at[m, k, j],
                lane_peer(j),
            )

        def exchange(m, k, i):
            lo, n = chunks[i]
            src, dst = ((gu_send, gu_recv), (h_send, h_recv))[k]
            return remote(
                src.at[m, lo : lo + n], dst.at[m, lo : lo + n], y_s.at[m, k, i], y_r.at[m, k, i],
                y_peer,
            )

        def give_back(m, j):
            return remote(
                ret_send.at[m, j], ret_recv.at[m, j], r_s.at[m, j], r_r.at[m, j], lane_peer(j)
            )

        def give_scalars(m, j):
            return remote(
                sc_send.at[m, j], sc_recv.at[m, j], v_s.at[m, j], v_r.at[m, j], lane_peer(j)
            )

        def squares_copy():
            return remote(sq_send, sq_recv, q_s, q_r, y_peer)

        def section_copy():
            return remote(out.at[0, 0], sec_recv, c_s, c_r, (s - 1, t, x))

        started = []

        def start(copy):
            copy.start()
            started.append(copy)

        quarter = max(1, experts // 4)
        chunks = [(0, 2 * quarter), (3 * quarter, quarter), (2 * quarter, quarter)]
        order = js[3 * quarter :] + js[1 : 2 * quarter] + js[2 * quarter : 3 * quarter]

        height = max(8, experts)
        lane = lax.broadcasted_iota(jnp.int32, (tok, 128), 1)
        row = lax.broadcasted_iota(jnp.int32, (height, tok), 0)
        named = jnp.full((height, tok), experts, jnp.int32)
        for j in js:
            named = jnp.where(row == j, expert_at(j), named)
        later = (
            lax.broadcasted_iota(jnp.int32, (tok, tok), 0)
            < lax.broadcasted_iota(jnp.int32, (tok, tok), 1)
        ).astype(f32).astype(bf16)
        slot = lax.broadcasted_iota(jnp.int32, (capacity, tok), 0).astype(f32)
        for m in range(2):
            hit = jnp.zeros((height, tok), f32)
            weight = jnp.zeros((height, tok), f32)
            for k in range(top):
                same = (ids[0, m, k : k + 1, :] == named).astype(f32)
                hit = hit + same
                weight = weight + same * weights[0, m, k : k + 1, :]
            position = dot(hit.astype(bf16), later)
            for j in js:
                chosen = (position[j : j + 1] == slot).astype(f32) * hit[j : j + 1]
                choose[m, j] = chosen.astype(bf16)
                picked[m, j] = jnp.broadcast_to(
                    jnp.sum(chosen * weight[j : j + 1], axis=1, keepdims=True), (capacity, 128)
                )
        square = []
        for m in range(2):
            values = saved[0, m].astype(f32)
            square.append(jnp.sum(values * values, axis=1, keepdims=True))
        sq_send[...] = jnp.where(lane < 64, square[0], square[1])

        def pack(m, k, value):
            packed = dot(choose[m].reshape(experts * capacity, tok), value)
            packed = packed.reshape(experts, capacity, feat)
            if k == 1:
                packed = packed * picked[m][:, :, :1]
            packed = packed.astype(bf16)
            rows[m, k, 0] = packed[0]
            rows_out[m, k, 1:] = packed[1:]

        for load in loads:
            load.wait()
        neighbours = (s > 0).astype(jnp.int32) + (s < sections - 1).astype(jnp.int32)
        pl.semaphore_wait(barrier, len(greet) + neighbours)

        start(squares_copy())
        pack(0, 1, cot_in[0])
        for j in order:
            start(direct(0, 1, j))
        for i in range(3):
            start(weight_copy(i))

        squares_copy().wait_recv()
        total = sq_send[...] + sq_recv[...]
        roots = [
            jnp.sqrt(total[:, 64 * m : 64 * m + 1] / model + epsilon) for m in range(2)
        ]

        def normed_of(m):
            return saved[0, m].astype(f32) / roots[m]

        def expert_input(m):
            return (normed_of(m) * gain[...]).astype(bf16)

        pack(0, 0, expert_input(0))
        for j in order:
            start(direct(0, 0, j))
        pack(1, 0, expert_input(1))

        @pl.when(s == 0)
        def _():
            for j in order:
                direct(1, 0, j).start()

        for i in range(3):
            weight_copy(i).wait_recv()

        def consume(m, k, i):
            lo, n = chunks[i]
            for j in range(max(1, lo), lo + n):
                direct(m, k, j).wait_recv()
            flat = rows[m, k, lo : lo + n].reshape(n * capacity, feat)
            if k == 0:
                done = dot(flat, wgu[...]).reshape(n, capacity, 4 * hid)
                part_gu[m, lo : lo + n] = done
                gu_send[m, lo : lo + n] = done.astype(bf16)
            else:
                done = contract_last(flat, wd[...]).reshape(n, capacity, 2 * hid)
                part_h[m, lo : lo + n] = done
                h_send[m, lo : lo + n] = done.astype(bf16)
            exchange(m, k, i).start()

        def produce(m, i):
            lo, n = chunks[i]
            exchange(m, 0, i).wait_recv()
            exchange(m, 1, i).wait_recv()
            ones = jnp.ones((8, 2 * hid), bf16)
            for j in range(lo, lo + n):
                both = part_gu[m, j] + gu_recv[m, j].astype(f32)
                hidden = part_h[m, j] + h_recv[m, j].astype(f32)
                gate, up = both[:, : 2 * hid], both[:, 2 * hid :]
                sigma = jax.nn.sigmoid(gate)
                grad_gate = hidden * up * (sigma * (1.0 + gate * (1.0 - sigma)))
                grad_up = hidden * (gate * sigma)
                grads[m, j, :, : 2 * hid] = grad_gate.astype(bf16)
                grads[m, j, :, 2 * hid :] = grad_up.astype(bf16)
                inner = (grad_gate * gate + grad_up * up).astype(bf16)
                scalars = contract_last(ones, inner)
                if j == 0:
                    sc_recv[m, j, :, :capacity] = scalars
                else:
                    sc_send[m, j, :, :capacity] = scalars
                    start(give_scalars(m, j))
            flat = grads[m, lo : lo + n].reshape(n * capacity, 4 * hid)
            done = contract_last(flat, wgu[...]).reshape(n, capacity, feat).astype(bf16)
            for j in range(lo, lo + n):
                if j == 0:
                    ret_recv[m, 0] = done[0]
                else:
                    ret_send[m, j] = done[j - lo]
                    start(give_back(m, j))

        def combine(m, incoming):
            for j in js[1:]:
                give_scalars(m, j).wait_recv()
            inner = jnp.zeros((tok, 8), f32)
            for j in js:
                inner = inner + lax.dot_general(
                    choose[m, j], sc_recv[m, j, :, :capacity].astype(bf16),
                    (((0,), (1,)), ((), ())), preferred_element_type=f32,
                )
            inner = inner[:, :1]
            for j in js[1:]:
                give_back(m, j).wait_recv()
            cot = contract_first(
                choose[m].reshape(experts * capacity, tok),
                ret_recv[m].reshape(experts * capacity, feat),
            )
            scaled = gain[...] * cot
            normed = normed_of(m)
            out[0, m] = (
                incoming + (scaled - normed * (inner / model)) / roots[m]
            ).astype(bf16)

        consume(0, 1, 1)
        consume(0, 1, 0)
        consume(0, 1, 2)
        consume(0, 0, 1)
        consume(0, 0, 0)
        consume(0, 0, 2)
        produce(0, 1)
        produce(0, 0)
        produce(0, 2)

        @pl.when(s == 0)
        def _():
            for i in (1, 0, 2):
                consume(1, 0, i)

        @pl.when(s > 0)
        def _():
            for j in order:
                direct(1, 0, j).start()

        @pl.when(s == sections - 1)
        def _():
            sec_recv[...] = loss_grad[...]
            pack(1, 1, sec_recv[...])
            for j in order:
                direct(1, 1, j).start()

        combine(0, cot_in[0].astype(f32))

        @pl.when(s > 0)
        def _():
            section_copy().start()
            for i in (1, 0, 2):
                consume(1, 0, i)

        @pl.when(s < sections - 1)
        def _():
            section_copy().wait_recv()
            pack(1, 1, sec_recv[...])
            for j in order:
                direct(1, 1, j).start()

        for i in (1, 0, 2):
            consume(1, 1, i)
        for i in (1, 0, 2):
            produce(1, i)
        combine(1, sec_recv[...].astype(f32))

        for copy in started:
            copy.wait_send()
        for j in js[1:]:
            for k in range(2):
                direct(1, k, j).wait_send()
        for m in range(2):
            for k in range(2):
                for i in range(3):
                    exchange(m, k, i).wait_send()

        @pl.when(s > 0)
        def _():
            section_copy().wait_send()

    return kernel


def solution(mesh):
    sections, tensors = mesh.shape["section"], mesh.shape["tensor"]
    experts = mesh.shape["expert"] // 2

    def local(saved, cot_in, loss_grad, ids, weights, gain, wg, wu, wd):
        tok, feat = saved.shape[2], saved.shape[3]
        hid = wg.shape[3]
        named = 3 * tok * ids.shape[3] // (2 * experts)
        cap = -(-named // 16) * 16
        vmem = pl.BlockSpec(memory_space=pltpu.VMEM)
        hbm = pl.BlockSpec(memory_space=pl.ANY)
        dma = pltpu.SemaphoreType.DMA
        scratch = [
            pltpu.VMEM((feat, 4 * hid), bf16), pltpu.VMEM((2 * hid, feat), bf16), dma((3,)),
            pltpu.VMEM((2, experts, cap, tok), bf16), pltpu.VMEM((2, experts, cap, 128), f32),
            pltpu.VMEM((2, 2, experts, cap, feat), bf16),
            pltpu.VMEM((2, 2, experts, cap, feat), bf16),
            pltpu.VMEM((2, experts, cap, 4 * hid), f32),
            pltpu.VMEM((2, experts, cap, 2 * hid), f32),
            pltpu.VMEM((2, experts, cap, 4 * hid), bf16),
            pltpu.VMEM((2, experts, cap, 4 * hid), bf16),
            pltpu.VMEM((2, experts, cap, 2 * hid), bf16),
            pltpu.VMEM((2, experts, cap, 2 * hid), bf16),
            pltpu.VMEM((2, experts, cap, 4 * hid), bf16),
            pltpu.VMEM((2, experts, cap, feat), bf16),
            pltpu.VMEM((2, experts, cap, feat), bf16),
            pltpu.VMEM((2, experts, 8, 128), f32), pltpu.VMEM((2, experts, 8, 128), f32),
            pltpu.VMEM((tok, 128), f32), pltpu.VMEM((tok, 128), f32),
            pltpu.VMEM((tok, feat), bf16),
        ]
        pair = [dma, dma]
        scratch += [dma((3,))] * 2 + [dma((2, 2, experts))] * 2 + [dma((2, 2, 3))] * 2
        scratch += [dma((2, experts))] * 4 + pair + pair
        return pl.pallas_call(
            make_kernel(sections, tensors, experts, cap),
            out_shape=jax.ShapeDtypeStruct((1, 2, tok, feat), bf16),
            in_specs=[vmem] * 6 + [hbm] * 3,
            out_specs=vmem,
            scratch_shapes=scratch,
            compiler_params=pltpu.CompilerParams(
                collective_id=0, has_side_effects=True, vmem_limit_bytes=62 * 1024 * 1024
            ),
            name="expert_back",
        )(
            saved, cot_in, loss_grad, ids.transpose(0, 1, 3, 2), weights.transpose(0, 1, 3, 2),
            gain, wg, wu, wd,
        )

    in_specs = (
        P("section", None, "expert", "tensor"),
        P("section", "expert", "tensor"),
        P("expert", "tensor"),
        P("section", None, "expert", None),
        P("section", None, "expert", None),
        P("section", "tensor"),
        P("section", "expert", "tensor", None),
        P("section", "expert", "tensor", None),
        P("section", "expert", None, "tensor"),
    )
    out_specs = P("section", None, "expert", "tensor")
    return jax.shard_map(local, mesh=mesh, in_specs=in_specs, out_specs=out_specs, check_vma=False)
```

time: 91 us -> 78.1 us (0.86)
  the two profiles are of different devices: /device:TPU:0 before, /device:TPU:2 now
where the time goes in v1:
time: 78.1 us; the launch traced here: 77.9 us
  Pallas kernels  76.2 us (98%)
  local copies, waits for them, and re-layouts  1.67 us (2%)
    pallas_call x1, Pallas kernels, local(): pl.pallas_call(make_kernel(sections, tensors, experts, cap), out_shape=ja...  76.2 us
    unnamed x1, local copies, waits for them, and re-layouts  1.67 us

profile of v1, /device:TPU:2, one launch (start us, length us, event | category | flops | bytes accessed | tf_op | source)
XLA Modules:
  0.0 77.9 jit_solution(2976171780737201131)
XLA Ops:
  0.0 76.2 %expert_back.1 = bf16[1,2,64,1024]{3,2,1,0:T(8,128)(2,1)} custom-call(bf16[1,2,64,1024]{3,2,1,0:T(8,128)(2,1)} %saved.1, bf16[1,64,1024]{2,1,0:T(8,128)(2,1)} %cot_in.1, bf16[64,1024]{1,0:T(8,128)(2,1)} %loss_grad.1, s32[1,2,2,64]{3,2,1,0:T(2,128)} %bitcast.2, f32[1,2,2,64]{3,2,1,0:T(2,128)} %bitcast.3, f32[1,1024]{1,0:T(1,128)} %gain.1, ...), custom_call_target="tpu_custom_call" | custom-call | tf_op jit(solution)/shard_map/expert_back/pallas_call | solution.py:375
  76.2 1.7 %copy.11 = bf16[1,2,64,1024]{3,2,1,0:T(8,128)(2,1)} copy(bf16[1,2,64,1024]{3,2,1,0:T(8,128)(2,1)} %expert_back.1) | data formatting | bytes 524288

commit v2 on v1

--- a/solution.py
+++ b/solution.py
@@ -27,10 +27,14 @@
 
     def kernel(
         saved, cot_in, loss_grad, ids, weights, gain, wg_hbm, wu_hbm, wd_hbm, out,
-        wgu, wd, w_sem, choose, picked, rows_out, rows, part_gu, part_h,
+        wgu, wd, w_sem, choose, picked, rows_out, rows, part_gu, part_h, part_in,
         gu_send, gu_recv, h_send, h_recv, grads, ret_send, ret_recv,
         sc_send, sc_recv, sq_send, sq_recv, sec_recv,
+        xin, full_recv, ids_far, weights_far, choose_far, picked_far,
+        rows_up, ids_up, weights_up, choose_up, picked_up,
+        rows_top, ids_top, weights_top, choose_top, picked_top,
         w_s, w_r, d_s, d_r, y_s, y_r, r_s, r_r, v_s, v_r, q_s, q_r, c_s, c_r,
+        f_s, f_r, i_s, i_r, u_s, g_s, g_r, t_s, h_s, h_r,
     ):
         s = lax.axis_index("section")
         t = lax.axis_index("tensor")
@@ -51,7 +55,15 @@
         for load in loads:
             load.start()
 
+        line = experts == 4
+        relayed = ((False, True), (True, False)) if line else ((False, False), (False, False))
+        side = e // 2
+        inner = ((e + 1) // 2) % 2
+        far_slot = 3 - inner
+
         def expert_at(j):
+            if line and j >= 2:
+                return 2 - side if j == 2 else 3 * (1 - side)
             other, bit = e, 1
             while bit < experts:
                 if j & bit:
@@ -70,11 +82,15 @@
 
         @pl.when(s > 0)
         def _():
-            pl.semaphore_signal(barrier, inc=1, device_id=(s - 1, t, x), device_id_type=MESH)
+            for j in js:
+                below = (s - 1, t, 2 * expert_at(j) + q)
+                pl.semaphore_signal(barrier, inc=1, device_id=below, device_id_type=MESH)
 
         @pl.when(s < sections - 1)
         def _():
-            pl.semaphore_signal(barrier, inc=1, device_id=(s + 1, t, x), device_id_type=MESH)
+            for j in js:
+                above = (s + 1, t, 2 * expert_at(j) + q)
+                pl.semaphore_signal(barrier, inc=1, device_id=above, device_id_type=MESH)
 
         def remote(src, dst, send, recv, device):
             return pltpu.make_async_remote_copy(
@@ -90,11 +106,50 @@
             )[i]
             return remote(ref[0], ref[1], w_s.at[i], w_r.at[i], partner)
 
+        def landing(j):
+            return far_slot if line and j >= 2 else j
+
         def direct(m, k, j):
+            return remote(
+                rows_out.at[m, k, j], rows.at[m, k, landing(j)],
+                d_s.at[m, k, j], d_r.at[m, k, landing(j)], lane_peer(j),
+            )
+
+        def passed_on(m, k):
+            return remote(
+                rows_out.at[m, k, 2], rows.at[m, k, 2], d_s.at[m, k, 2], d_r.at[m, k, 2],
+                lane_peer(1),
+            )
+
+        def arrival(m, k, j):
             return remote(
                 rows_out.at[m, k, j], rows.at[m, k, j], d_s.at[m, k, j], d_r.at[m, k, j],
                 lane_peer(j),
             )
+
+        def whole(m, k):
+            src = xin.at[m] if k == 0 else (cot_in.at[0], sec_recv)[m]
+            return remote(src, full_recv.at[m, k], f_s.at[m, k], f_r.at[m, k], lane_peer(2))
+
+        def routes(i):
+            src, dst = ((ids, ids_far), (weights, weights_far))[i]
+            return remote(src, dst, i_s.at[i], i_r.at[i], lane_peer(2))
+
+        def send_rows(m, k):
+            if not relayed[m][k]:
+                for j in js[1:] if line else order:
+                    direct(m, k, j).start()
+                return
+
+            @pl.when(inner == 1)
+            def _():
+                whole(m, k).start()
+                direct(m, k, 1).start()
+
+            @pl.when(inner == 0)
+            def _():
+                for j in (1, 2, 3):
+                    direct(m, k, j).start()
 
         def exchange(m, k, i):
             lo, n = chunks[i]
@@ -106,10 +161,22 @@
 
         def give_back(m, j):
             return remote(
+                ret_send.at[m, j], ret_recv.at[m, landing(j)], r_s.at[m, j],
+                r_r.at[m, landing(j)], lane_peer(j),
+            )
+
+        def given_back(m, j):
+            return remote(
                 ret_send.at[m, j], ret_recv.at[m, j], r_s.at[m, j], r_r.at[m, j], lane_peer(j)
             )
 
         def give_scalars(m, j):
+            return remote(
+                sc_send.at[m, j], sc_recv.at[m, landing(j)], v_s.at[m, j],
+                v_r.at[m, landing(j)], lane_peer(j),
+            )
+
+        def given_scalars(m, j):
             return remote(
                 sc_send.at[m, j], sc_recv.at[m, j], v_s.at[m, j], v_r.at[m, j], lane_peer(j)
             )
@@ -119,6 +186,26 @@
 
         def section_copy():
             return remote(out.at[0, 0], sec_recv, c_s, c_r, (s - 1, t, x))
+
+        def descend(j):
+            return remote(
+                rows_up.at[j], rows.at[1, 1, landing(j)], u_s.at[j], d_r.at[1, 1, landing(j)],
+                (s - 1, t, 2 * expert_at(j) + q),
+            )
+
+        def ascend(j):
+            return remote(
+                rows_top.at[j], rows.at[1, 1, landing(j)], t_s.at[j], d_r.at[1, 1, landing(j)],
+                (s + 1, t, 2 * expert_at(j) + q),
+            )
+
+        def routes_top(i):
+            src, dst = ((ids, ids_top), (weights, weights_top))[i]
+            return remote(src, dst, h_s.at[i], h_r.at[i], (s - 1, t, x))
+
+        def routes_up(i):
+            src, dst = ((ids, ids_up), (weights, weights_up))[i]
+            return remote(src, dst, g_s.at[i], g_r.at[i], (s + 1, t, x))
 
         started = []
 
@@ -127,34 +214,40 @@
             started.append(copy)
 
         quarter = max(1, experts // 4)
-        chunks = [(0, 2 * quarter), (3 * quarter, quarter), (2 * quarter, quarter)]
+        near, far = js[1 : 2 * quarter], js[2 * quarter :]
+        chunks = [(i * quarter, quarter) for i in range(experts // quarter)]
         order = js[3 * quarter :] + js[1 : 2 * quarter] + js[2 * quarter : 3 * quarter]
 
-        height = max(8, experts)
         lane = lax.broadcasted_iota(jnp.int32, (tok, 128), 1)
-        row = lax.broadcasted_iota(jnp.int32, (height, tok), 0)
-        named = jnp.full((height, tok), experts, jnp.int32)
-        for j in js:
-            named = jnp.where(row == j, expert_at(j), named)
         later = (
             lax.broadcasted_iota(jnp.int32, (tok, tok), 0)
             < lax.broadcasted_iota(jnp.int32, (tok, tok), 1)
         ).astype(f32).astype(bf16)
         slot = lax.broadcasted_iota(jnp.int32, (capacity, tok), 0).astype(f32)
-        for m in range(2):
-            hit = jnp.zeros((height, tok), f32)
-            weight = jnp.zeros((height, tok), f32)
-            for k in range(top):
-                same = (ids[0, m, k : k + 1, :] == named).astype(f32)
-                hit = hit + same
-                weight = weight + same * weights[0, m, k : k + 1, :]
-            position = dot(hit.astype(bf16), later)
-            for j in js:
-                chosen = (position[j : j + 1] == slot).astype(f32) * hit[j : j + 1]
-                choose[m, j] = chosen.astype(bf16)
-                picked[m, j] = jnp.broadcast_to(
-                    jnp.sum(chosen * weight[j : j + 1], axis=1, keepdims=True), (capacity, 128)
-                )
+
+        def tables(ids, weights, count, choose, picked, batches=(0, 1)):
+            height = max(8, count)
+            row = lax.broadcasted_iota(jnp.int32, (height, tok), 0)
+            named = jnp.full((height, tok), experts, jnp.int32)
+            for j in range(count):
+                named = jnp.where(row == j, expert_at(j), named)
+            for m in batches:
+                hit = jnp.zeros((height, tok), f32)
+                weight = jnp.zeros((height, tok), f32)
+                for k in range(top):
+                    same = (ids[0, m, k : k + 1, :] == named).astype(f32)
+                    hit = hit + same
+                    weight = weight + same * weights[0, m, k : k + 1, :]
+                position = dot(hit.astype(bf16), later)
+                for j in range(count):
+                    chosen = (position[j : j + 1] == slot).astype(f32) * hit[j : j + 1]
+                    choose[m, j] = chosen.astype(bf16)
+                    picked[m, j] = jnp.broadcast_to(
+                        jnp.sum(chosen * weight[j : j + 1], axis=1, keepdims=True),
+                        (capacity, 128),
+                    )
+
+        tables(ids, weights, experts, choose, picked)
         square = []
         for m in range(2):
             values = saved[0, m].astype(f32)
@@ -170,17 +263,67 @@
             rows[m, k, 0] = packed[0]
             rows_out[m, k, 1:] = packed[1:]
 
+        def pack_for(choose, picked, dst, value):
+            low = far[0] if dst is rows_up else 1
+            packed = dot(choose[1, low:].reshape((experts - low) * capacity, tok), value)
+            packed = packed.reshape(experts - low, capacity, feat) * picked[1, low:][:, :, :1]
+            dst[low:] = packed.astype(bf16)
+
+        def pack_near(value):
+            high = far[0]
+            packed = dot(choose[1, :high].reshape(high * capacity, tok), value)
+            packed = packed.reshape(high, capacity, feat) * picked[1, :high][:, :, :1]
+            packed = packed.astype(bf16)
+            rows[1, 1, 0] = packed[0]
+            rows_out[1, 1, 1:high] = packed[1:]
+
         for load in loads:
             load.wait()
         neighbours = (s > 0).astype(jnp.int32) + (s < sections - 1).astype(jnp.int32)
-        pl.semaphore_wait(barrier, len(greet) + neighbours)
+        pl.semaphore_wait(barrier, len(greet) + experts * neighbours)
 
         start(squares_copy())
-        pack(0, 1, cot_in[0])
-        for j in order:
-            start(direct(0, 1, j))
         for i in range(3):
             start(weight_copy(i))
+        if line:
+
+            @pl.when(inner == 1)
+            def _():
+                for i in range(2):
+                    routes(i).start()
+
+        @pl.when(s < sections - 1)
+        def _():
+            for i in range(2):
+                routes_up(i).start()
+
+        @pl.when(s == sections - 1)
+        def _():
+            sec_recv[...] = loss_grad[...]
+            for i in range(2):
+                routes_top(i).start()
+
+        pack(0, 1, cot_in[0])
+        send_rows(0, 1)
+        if line:
+
+            @pl.when(inner == 1)
+            def _():
+                for i in range(2):
+                    routes(i).wait_recv()
+                tables(ids_far, weights_far, 2, choose_far, picked_far)
+
+        @pl.when(s > 0)
+        def _():
+            for i in range(2):
+                routes_up(i).wait_recv()
+            tables(ids_up, weights_up, experts, choose_up, picked_up, (1,))
+
+        @pl.when(s == sections - 2)
+        def _():
+            for i in range(2):
+                routes_top(i).wait_recv()
+            tables(ids_top, weights_top, experts, choose_top, picked_top, (1,))
 
         squares_copy().wait_recv()
         total = sq_send[...] + sq_recv[...]
@@ -191,26 +334,45 @@
         def normed_of(m):
             return saved[0, m].astype(f32) / roots[m]
 
-        def expert_input(m):
-            return (normed_of(m) * gain[...]).astype(bf16)
-
-        pack(0, 0, expert_input(0))
-        for j in order:
-            start(direct(0, 0, j))
-        pack(1, 0, expert_input(1))
-
-        @pl.when(s == 0)
-        def _():
-            for j in order:
-                direct(1, 0, j).start()
+        for m in range(2):
+            xin[m] = (normed_of(m) * gain[...]).astype(bf16)
+            pack(m, 0, xin[m])
+            if m == 0:
+                send_rows(0, 0)
 
         for i in range(3):
             weight_copy(i).wait_recv()
+
+        def relay(m, k):
+            if not relayed[m][k]:
+                return
+
+            @pl.when(inner == 1)
+            def _():
+                whole(m, k).wait_recv()
+                packed = dot(choose_far[m].reshape(2 * capacity, tok), full_recv[m, k])
+                packed = packed.reshape(2, capacity, feat)
+                if k == 1:
+                    packed = packed * picked_far[m][:, :, :1]
+                packed = packed.astype(bf16)
+                rows_out[m, k, 2] = packed[1]
+                passed_on(m, k).start()
+                rows[m, k, 2] = packed[0]
+
+        def receive(m, k, j):
+            if relayed[m][k] and j == 2:
+
+                @pl.when(inner == 0)
+                def _():
+                    arrival(m, k, j).wait_recv()
+
+            else:
+                arrival(m, k, j).wait_recv()
 
         def consume(m, k, i):
             lo, n = chunks[i]
             for j in range(max(1, lo), lo + n):
-                direct(m, k, j).wait_recv()
+                receive(m, k, j)
             flat = rows[m, k, lo : lo + n].reshape(n * capacity, feat)
             if k == 0:
                 done = dot(flat, wgu[...]).reshape(n, capacity, 4 * hid)
@@ -222,39 +384,48 @@
                 h_send[m, lo : lo + n] = done.astype(bf16)
             exchange(m, k, i).start()
 
-        def produce(m, i):
+        def prepare(m, i):
             lo, n = chunks[i]
             exchange(m, 0, i).wait_recv()
-            exchange(m, 1, i).wait_recv()
-            ones = jnp.ones((8, 2 * hid), bf16)
             for j in range(lo, lo + n):
                 both = part_gu[m, j] + gu_recv[m, j].astype(f32)
-                hidden = part_h[m, j] + h_recv[m, j].astype(f32)
                 gate, up = both[:, : 2 * hid], both[:, 2 * hid :]
                 sigma = jax.nn.sigmoid(gate)
-                grad_gate = hidden * up * (sigma * (1.0 + gate * (1.0 - sigma)))
-                grad_up = hidden * (gate * sigma)
-                grads[m, j, :, : 2 * hid] = grad_gate.astype(bf16)
-                grads[m, j, :, 2 * hid :] = grad_up.astype(bf16)
-                inner = (grad_gate * gate + grad_up * up).astype(bf16)
-                scalars = contract_last(ones, inner)
+                for_up = gate * sigma
+                for_gate = up * (sigma * (1.0 + gate * (1.0 - sigma)))
+                part_gu[m, j, :, : 2 * hid] = for_gate
+                part_gu[m, j, :, 2 * hid :] = for_up
+                part_in[m, j] = for_gate * gate + for_up * up
+
+        def produce(m, *group):
+            for i in group:
+                exchange(m, 1, i).wait_recv()
+            ones = jnp.ones((8, 2 * hid), bf16)
+            first, count = chunks[min(group)][0], sum(chunks[i][1] for i in group)
+            for j in range(first, first + count):
+                hidden = part_h[m, j] + h_recv[m, j].astype(f32)
+                for a in (0, 2 * hid):
+                    grads[m, j, :, a : a + 2 * hid] = (
+                        hidden * part_gu[m, j, :, a : a + 2 * hid]
+                    ).astype(bf16)
+                scalars = contract_last(ones, (hidden * part_in[m, j]).astype(bf16))
                 if j == 0:
                     sc_recv[m, j, :, :capacity] = scalars
                 else:
                     sc_send[m, j, :, :capacity] = scalars
                     start(give_scalars(m, j))
-            flat = grads[m, lo : lo + n].reshape(n * capacity, 4 * hid)
-            done = contract_last(flat, wgu[...]).reshape(n, capacity, feat).astype(bf16)
-            for j in range(lo, lo + n):
+            flat = grads[m, first : first + count].reshape(count * capacity, 4 * hid)
+            done = contract_last(flat, wgu[...]).reshape(count, capacity, feat).astype(bf16)
+            for j in range(first, first + count)[::-1]:
                 if j == 0:
                     ret_recv[m, 0] = done[0]
                 else:
-                    ret_send[m, j] = done[j - lo]
+                    ret_send[m, j] = done[j - first]
                     start(give_back(m, j))
 
         def combine(m, incoming):
             for j in js[1:]:
-                give_scalars(m, j).wait_recv()
+                given_scalars(m, j).wait_recv()
             inner = jnp.zeros((tok, 8), f32)
             for j in js:
                 inner = inner + lax.dot_general(
@@ -263,7 +434,7 @@
                 )
             inner = inner[:, :1]
             for j in js[1:]:
-                give_back(m, j).wait_recv()
+                given_back(m, j).wait_recv()
             cot = contract_first(
                 choose[m].reshape(experts * capacity, tok),
                 ret_recv[m].reshape(experts * capacity, feat),
@@ -274,67 +445,127 @@
                 incoming + (scaled - normed * (inner / model)) / roots[m]
             ).astype(bf16)
 
+        last = len(chunks)
+        consume(0, 1, 0)
+        consume(0, 0, 0)
+        relay(0, 1)
         consume(0, 1, 1)
-        consume(0, 1, 0)
-        consume(0, 1, 2)
         consume(0, 0, 1)
-        consume(0, 0, 0)
-        consume(0, 0, 2)
+        for i in range(2, last):
+            consume(0, 1, i)
+        for i in range(2, last):
+            consume(0, 0, i)
+        send_rows(1, 0)
+        @pl.when(s == sections - 2)
+        def _():
+            pack_for(choose_top, picked_top, rows_top, loss_grad[...])
+            for j in js[1:]:
+                ascend(j).start()
+
+        prepare(0, 0)
+        produce(0, 0)
+        prepare(0, 1)
         produce(0, 1)
-        produce(0, 0)
+        prepare(0, 2)
         produce(0, 2)
+        relay(1, 0)
+        prepare(0, 3)
+        produce(0, 3)
+        for i in range(last):
+            consume(1, 0, i)
+
+        @pl.when(s > 0)
+        def _():
+            combine(0, cot_in[0].astype(f32))
+            section_copy().start()
+            pack_for(choose_up, picked_up, rows_up, out[0, 0])
+            for j in far:
+                descend(j).start()
+
+        @pl.when(s < sections - 1)
+        def _():
+            section_copy().wait_recv()
+            pack_near(sec_recv[...])
+            for j in near:
+                direct(1, 1, j).start()
+
+        @pl.when(s == sections - 1)
+        def _():
+            pack_near(sec_recv[...])
+
+        consume(1, 1, 0)
+        consume(1, 1, 2)
+        consume(1, 1, 3)
+        consume(1, 1, 1)
+        prepare(1, 2)
+        prepare(1, 3)
+        prepare(1, 0)
+        prepare(1, 1)
+        produce(1, 2, 3)
+        produce(1, 0, 1)
 
         @pl.when(s == 0)
         def _():
-            for i in (1, 0, 2):
-                consume(1, 0, i)
-
-        @pl.when(s > 0)
-        def _():
-            for j in order:
-                direct(1, 0, j).start()
-
-        @pl.when(s == sections - 1)
-        def _():
-            sec_recv[...] = loss_grad[...]
-            pack(1, 1, sec_recv[...])
-            for j in order:
-                direct(1, 1, j).start()
-
-        combine(0, cot_in[0].astype(f32))
-
-        @pl.when(s > 0)
-        def _():
-            section_copy().start()
-            for i in (1, 0, 2):
-                consume(1, 0, i)
-
-        @pl.when(s < sections - 1)
-        def _():
-            section_copy().wait_recv()
-            pack(1, 1, sec_recv[...])
-            for j in order:
-                direct(1, 1, j).start()
-
-        for i in (1, 0, 2):
-            consume(1, 1, i)
-        for i in (1, 0, 2):
-            produce(1, i)
+            combine(0, cot_in[0].astype(f32))
+
         combine(1, sec_recv[...].astype(f32))
 
         for copy in started:
             copy.wait_send()
-        for j in js[1:]:
-            for k in range(2):
-                direct(1, k, j).wait_send()
         for m in range(2):
             for k in range(2):
-                for i in range(3):
+                for i in range(last):
                     exchange(m, k, i).wait_send()
+                if m == 1 and k == 1:
+
+                    @pl.when(s < sections - 1)
+                    def _():
+                        for j in near:
+                            direct(1, 1, j).wait_send()
+
+                    continue
+                if not relayed[m][k]:
+                    for j in js[1:]:
+                        direct(m, k, j).wait_send()
+                    continue
+                direct(m, k, 1).wait_send()
+                direct(m, k, 2).wait_send()
+
+                @pl.when(inner == 1)
+                def _():
+                    whole(m, k).wait_send()
+
+                @pl.when(inner == 0)
+                def _():
+                    direct(m, k, 3).wait_send()
+
+        if line:
+
+            @pl.when(inner == 1)
+            def _():
+                for i in range(2):
+                    routes(i).wait_send()
 
         @pl.when(s > 0)
         def _():
             section_copy().wait_send()
+            for j in far:
+                descend(j).wait_send()
+
+        @pl.when(s == sections - 2)
+        def _():
+            for j in js[1:]:
+                ascend(j).wait_send()
+
+        @pl.when(s == sections - 1)
+        def _():
+            for i in range(2):
+                routes_top(i).wait_send()
+
+        @pl.when(s < sections - 1)
+        def _():
+            for i in range(2):
+                routes_up(i).wait_send()
 
     return kernel
 
@@ -358,6 +589,7 @@
             pltpu.VMEM((2, 2, experts, cap, feat), bf16),
             pltpu.VMEM((2, experts, cap, 4 * hid), f32),
             pltpu.VMEM((2, experts, cap, 2 * hid), f32),
+            pltpu.VMEM((2, experts, cap, 2 * hid), f32),
             pltpu.VMEM((2, experts, cap, 4 * hid), bf16),
             pltpu.VMEM((2, experts, cap, 4 * hid), bf16),
             pltpu.VMEM((2, experts, cap, 2 * hid), bf16),
@@ -368,10 +600,20 @@
             pltpu.VMEM((2, experts, 8, 128), f32), pltpu.VMEM((2, experts, 8, 128), f32),
             pltpu.VMEM((tok, 128), f32), pltpu.VMEM((tok, 128), f32),
             pltpu.VMEM((tok, feat), bf16),
+            pltpu.VMEM((2, tok, feat), bf16), pltpu.VMEM((2, 2, tok, feat), bf16),
+            pltpu.VMEM((1, 2, ids.shape[3], tok), jnp.int32),
+            pltpu.VMEM((1, 2, ids.shape[3], tok), f32),
+            pltpu.VMEM((2, 2, cap, tok), bf16), pltpu.VMEM((2, 2, cap, 128), f32),
+            pltpu.VMEM((experts, cap, feat), bf16),
+            pltpu.VMEM((1, 2, ids.shape[3], tok), jnp.int32),
+            pltpu.VMEM((1, 2, ids.shape[3], tok), f32),
+            pltpu.VMEM((2, experts, cap, tok), bf16), pltpu.VMEM((2, experts, cap, 128), f32),
         ]
+        scratch += scratch[-5:]
         pair = [dma, dma]
-        scratch += [dma((3,))] * 2 + [dma((2, 2, experts))] * 2 + [dma((2, 2, 3))] * 2
-        scratch += [dma((2, experts))] * 4 + pair + pair
+        scratch += [dma((3,))] * 2 + [dma((2, 2, experts))] * 2 + [dma((2, 2, min(experts, 4)))] * 2
+        scratch += [dma((2, experts))] * 4 + pair + pair + [dma((2, 2))] * 2 + [dma((2,))] * 2
+        scratch += ([dma((experts,))] + [dma((2,))] * 2) * 2
         return pl.pallas_call(
             make_kernel(sections, tensors, experts, cap),
             out_shape=jax.ShapeDtypeStruct((1, 2, tok, feat), bf16),

time: 78.1 us -> 66.8 us (0.86)
  the two profiles are of different devices: /device:TPU:2 before, /device:TPU:0 now
where the time goes in v2:
time: 66.8 us; the launch traced here: 66.6 us
  Pallas kernels  64.9 us (97%)
  local copies, waits for them, and re-layouts  1.67 us (2%)
    pallas_call x1, Pallas kernels, local(): pl.pallas_call(make_kernel(sections, tensors, experts, cap), out_shape=ja...  64.9 us
    unnamed x1, local copies, waits for them, and re-layouts  1.67 us

profile of v2, /device:TPU:0, one launch (start us, length us, event | category | flops | bytes accessed | tf_op | source)
XLA Modules:
  0.0 66.6 jit_solution(2034341204005036197)
XLA Ops:
  0.0 64.9 %expert_back.1 = bf16[1,2,64,1024]{3,2,1,0:T(8,128)(2,1)} custom-call(bf16[1,2,64,1024]{3,2,1,0:T(8,128)(2,1)} %saved.1, bf16[1,64,1024]{2,1,0:T(8,128)(2,1)} %cot_in.1, bf16[64,1024]{1,0:T(8,128)(2,1)} %loss_grad.1, s32[1,2,2,64]{3,2,1,0:T(2,128)} %bitcast.2, f32[1,2,2,64]{3,2,1,0:T(2,128)} %bitcast.3, f32[1,1024]{1,0:T(1,128)} %gain.1, ...), custom_call_target="tpu_custom_call" | custom-call | tf_op jit(solution)/shard_map/expert_back/pallas_call | solution.py:617
  64.9 1.7 %copy.11 = bf16[1,2,64,1024]{3,2,1,0:T(8,128)(2,1)} copy(bf16[1,2,64,1024]{3,2,1,0:T(8,128)(2,1)} %expert_back.1) | data formatting | bytes 524288

commit v3 on v2

--- a/solution.py
+++ b/solution.py
@@ -247,7 +247,7 @@
                         (capacity, 128),
                     )
 
-        tables(ids, weights, experts, choose, picked)
+        tables(ids, weights, experts, choose, picked, (0,))
         square = []
         for m in range(2):
             values = saved[0, m].astype(f32)
@@ -305,6 +305,7 @@
 
         pack(0, 1, cot_in[0])
         send_rows(0, 1)
+        tables(ids, weights, experts, choose, picked, (1,))
         if line:
 
             @pl.when(inner == 1)
@@ -453,9 +454,9 @@
         consume(0, 0, 1)
         for i in range(2, last):
             consume(0, 1, i)
+        send_rows(1, 0)
         for i in range(2, last):
             consume(0, 0, i)
-        send_rows(1, 0)
         @pl.when(s == sections - 2)
         def _():
             pack_for(choose_top, picked_top, rows_top, loss_grad[...])

time: 66.8 us -> 66.8 us (level)
  no operation moved by 1% of the time
where the time goes in v3:
time: 66.8 us; the launch traced here: 66.6 us
  Pallas kernels  64.9 us (97%)
  local copies, waits for them, and re-layouts  1.67 us (2%)
    pallas_call x1, Pallas kernels, local(): pl.pallas_call(make_kernel(sections, tensors, experts, cap), out_shape=ja...  64.9 us
    unnamed x1, local copies, waits for them, and re-layouts  1.67 us

profile of v3, /device:TPU:0, one launch (start us, length us, event | category | flops | bytes accessed | tf_op | source)
XLA Modules:
  0.0 66.6 jit_solution(3938670195922536148)
XLA Ops:
  0.0 64.9 %expert_back.1 = bf16[1,2,64,1024]{3,2,1,0:T(8,128)(2,1)} custom-call(bf16[1,2,64,1024]{3,2,1,0:T(8,128)(2,1)} %saved.1, bf16[1,64,1024]{2,1,0:T(8,128)(2,1)} %cot_in.1, bf16[64,1024]{1,0:T(8,128)(2,1)} %loss_grad.1, s32[1,2,2,64]{3,2,1,0:T(2,128)} %bitcast.2, f32[1,2,2,64]{3,2,1,0:T(2,128)} %bitcast.3, f32[1,1024]{1,0:T(1,128)} %gain.1, ...), custom_call_target="tpu_custom_call" | custom-call | tf_op jit(solution)/shard_map/expert_back/pallas_call | solution.py:618
  64.9 1.7 %copy.11 = bf16[1,2,64,1024]{3,2,1,0:T(8,128)(2,1)} copy(bf16[1,2,64,1024]{3,2,1,0:T(8,128)(2,1)} %expert_back.1) | data formatting | bytes 524288
